TPU v7x, 32 devices: a whole 2x2x4 slice. The times are simulated.
32 devices in a mesh: fsdp: 4 (over y, x), tp: 8 (over z, core).
Axes of the slice: x: 2, y: 2, z: 4, core: 2. Of those that a mesh axis runs over, the one named last changes fastest.
Arguments:
- tokens: bfloat16 [1024, 8192], P('fsdp', 'tp'), may hold values from -6 to 6
- out_grad: bfloat16 [1024, 8192], P('fsdp', 'tp'), may hold values from -6 to 6
- gate_weight: bfloat16 [8192, 1024], P('fsdp', 'tp'), may hold values from -0.0625 to 0.0625
- up_weight: bfloat16 [8192, 1024], P('fsdp', 'tp'), may hold values from -0.0625 to 0.0625
- down_weight: bfloat16 [1024, 8192], P('tp', 'fsdp'), may hold values from -0.1875 to 0.1875
Outputs:
- input_grad: bfloat16 [1024, 8192], P('fsdp', 'tp')
- gate_grad: float32 [8192, 1024], P('fsdp', 'tp')
- up_grad: float32 [8192, 1024], P('fsdp', 'tp')
- down_grad: float32 [1024, 8192], P('tp', 'fsdp')
All inputs are finite; a program needn't handle non-finite values.
Results may differ from a plain program's by a relative error of at most 0.0023.
Values may be sent and summed in bfloat16 or wider, within the bound.
A program may use at most 128 MiB of HBM per device.

v0:
```python
import math
import jax
import jax.numpy as jnp
from jax import lax
from jax.sharding import PartitionSpec as P


def over_all(shard, axis, dim, absorb, state):
    everything = jax.tree.map(lambda a: lax.all_gather(a, axis, axis=dim, tiled=True), shard)
    return absorb(state, everything, jnp.int32(0))


def own_rows(portion, rows, axis):
    count = rows * lax.axis_size(axis)
    return lax.psum_scatter(portion(jnp.int32(0), count), axis, scatter_dimension=0, tiled=True)


def column_term(left, right, start, count, factor):
    block = lax.dynamic_slice_in_dim(left, start, count, 1)
    product = lax.dot_general(
        block, right, (((0,), (0,)), ((), ())), preferred_element_type=jnp.float32
    )
    return product * factor


def body(tokens, out_grad, gate_weight, up_weight, down_weight):
    factor = 1.0 / math.sqrt(tokens.shape[0] * lax.axis_size("fsdp"))
    whole = lax.all_gather(tokens, "tp", axis=1, tiled=True)
    grads = lax.all_gather(out_grad, "tp", axis=1, tiled=True)
    gate_full, up_full = (
        lax.all_gather(gate_weight, "fsdp", axis=0, tiled=True),
        lax.all_gather(up_weight, "fsdp", axis=0, tiled=True),
    )
    gate = jnp.dot(whole, gate_full, preferred_element_type=jnp.float32)
    up = jnp.dot(whole, up_full, preferred_element_type=jnp.float32)

    def add_down(total, piece, start):
        columns = lax.dynamic_slice_in_dim(grads, start, piece.shape[1], 1)
        return total + lax.dot_general(
            columns, piece, (((1,), (1,)), ((), ())), preferred_element_type=jnp.float32
        )

    initial = jnp.zeros((whole.shape[0], down_weight.shape[0]), jnp.float32)
    hidden_grad = over_all(down_weight, "fsdp", 1, add_down, initial)
    squashed = jax.nn.sigmoid(gate)
    activated = gate * squashed
    slope = squashed * (1.0 + gate * (1.0 - squashed))
    hidden = (activated * up).astype(jnp.bfloat16)
    gate_delta = (hidden_grad * up * slope).astype(jnp.bfloat16)
    up_delta = (hidden_grad * activated).astype(jnp.bfloat16)
    partial_term = jnp.dot(gate_delta, gate_full.T, preferred_element_type=jnp.float32)
    partial_term = partial_term + jnp.dot(up_delta, up_full.T, preferred_element_type=jnp.float32)
    input_grad = lax.psum_scatter(partial_term, "tp", scatter_dimension=1, tiled=True).astype(
        jnp.bfloat16
    )
    rows_here = gate_weight.shape[0]

    def joint_term(start, count):
        return jnp.concatenate(
            [
                column_term(whole, gate_delta, start, count, factor),
                column_term(whole, up_delta, start, count, factor),
                column_term(grads, hidden, start, count, factor),
            ],
            axis=1,
        )

    summed = own_rows(joint_term, rows_here, "fsdp")
    width = gate_delta.shape[1]
    gate_grad = summed[:, :width]
    up_grad = summed[:, width : 2 * width]
    down_grad = summed[:, 2 * width :].T
    return (input_grad, gate_grad, up_grad, down_grad)


def solution(mesh):
    return jax.shard_map(
        body,
        mesh=mesh,
        in_specs=(
            P("fsdp", "tp"),
            P("fsdp", "tp"),
            P("fsdp", "tp"),
            P("fsdp", "tp"),
            P("tp", "fsdp"),
        ),
        out_specs=(P("fsdp", "tp"), P("fsdp", "tp"), P("fsdp", "tp"), P("tp", "fsdp")),
        check_vma=False,
    )
```

profile of v0, /device:TPU:0, one launch (start us, length us, event | category | flops | bytes accessed | tf_op | source)
XLA Modules:
  0.0 450.8 jit_solution(9459281939705098741)
XLA Ops:
  7.2 0.0 all-gather.14.cloned.1.call-start
  7.2 0.7 all-gather.14.cloned.1.call-update
  7.9 0.0 all-gather.10.cloned.1.call-start
  7.9 0.7 all-gather.10.cloned.1.call-update
  8.6 0.0 all-gather.12.cloned.1.call-start
  8.7 0.7 all-gather.12.cloned.1.call-update
  9.4 0.0 all-gather.8.cloned.1.call-start
  9.4 0.5 all-gather.8.cloned.1.call-update
  10.0 0.0 all-gather.6.cloned.1.call-start
  10.0 0.5 all-gather.6.cloned.1.call-update
  10.5 0.0 reduce-scatter.3.cloned.1.call-start
  10.6 37.2 %all-gather.14.cloned.1.call-done = bf16[8192,128]{1,0:T(8,128)(2,1)} async-done(((bf16[2048,128]{1,0:T(8,128)(2,1)}), bf16[8192,128]{1,0:T(8,128)(2,1)}) %all-gather.14.cloned.1.call-update) | async-done | bytes 2097168 | tf_op jit(solution)/shard_map/all_gather | solution.py:31
  47.8 48.5 %all-gather.10.cloned.1.call-done = bf16[256,8192]{1,0:T(8,128)(2,1)} async-done(((bf16[256,1024]{1,0:T(8,128)(2,1)}), bf16[256,8192]{1,0:T(8,128)(2,1)}) %all-gather.10.cloned.1.call-update) | async-done | bytes 4194320 | tf_op jit(solution)/shard_map/all_gather | solution.py:28
  96.3 4.1 fusion.7
  100.4 31.8 %all-gather.12.cloned.1.call-done = bf16[8192,128]{1,0:T(8,128)(2,1)} async-done(((bf16[2048,128]{1,0:T(8,128)(2,1)}), bf16[8192,128]{1,0:T(8,128)(2,1)}) %all-gather.12.cloned.1.call-update) | async-done | bytes 2097168 | tf_op jit(solution)/shard_map/all_gather | solution.py:32
  132.1 4.1 fusion.6
  136.2 0.0 copy-start.1
  136.2 32.8 %all-gather.8.cloned.1.call-done = bf16[128,8192]{1,0:T(8,128)(2,1)} async-done(((bf16[128,2048]{1,0:T(8,128)(2,1)}), bf16[128,8192]{1,0:T(8,128)(2,1)}) %all-gather.8.cloned.1.call-update) | async-done | bytes 2097168 | tf_op jit(solution)/shard_map/all_gather | solution.py:9
  169.0 48.4 %all-gather.6.cloned.1.call-done = bf16[256,8192]{1,0:T(8,128)(2,1)} async-done(((bf16[256,1024]{1,0:T(8,128)(2,1)}), bf16[256,8192]{1,0:T(8,128)(2,1)}) %all-gather.6.cloned.1.call-update) | async-done | bytes 4194320 | tf_op jit(solution)/shard_map/all_gather | solution.py:29
  217.4 4.1 multiply_convert_fusion.1
  221.5 0.0 copy-done.1
  221.5 0.0 copy-start.2
  221.5 1.3 fusion.8
  222.8 0.3 copy-done.2
  223.1 4.5 convolution_add_fusion
  227.6 0.0 reduce-scatter.3.cloned.1.call-update
  227.6 0.0 reduce-scatter.5.cloned.1.call-start
  227.6 0.0 copy-start
  227.6 3.1 fusion.1
  230.8 0.3 copy-done
  231.1 0.0 copy-start.3
  231.1 0.8 fusion.2
  231.9 2.1 copy-done.3
  234.0 0.8 fusion
  234.8 5.0 %pad_maximum_fusion = f32[8192,384]{0,1:T(8,128)} fusion(f32[8192,128]{0,1:T(8,128)S(1)} %fusion, f32[8192,128]{0,1:T(8,128)S(1)} %fusion.1, f32[8192,128]{0,1:T(8,128)S(1)} %fusion.2), kind=kLoop, calls=%fused_computation | loop fusion | flops 6291456 | bytes 25165824 | tf_op jit(solution)/shard_map/concatenate | solution.py:59
  239.8 0.0 reduce-scatter.5.cloned.1.call-update
  239.9 76.2 %reduce-scatter.3.cloned.1.call-done = f32[256,1024]{1,0:T(8,128)} async-done(((f32[256,8192]{1,0:T(8,128)}), f32[256,1024]{1,0:T(8,128)}) %reduce-scatter.3.cloned.1.call-update) | async-done | bytes 1048592 | tf_op jit(solution)/shard_map/reduce_scatter | solution.py:53
  316.1 2.1 convert_element_type.14
  318.2 120.1 %reduce-scatter.5.cloned.1.call-done = f32[2048,384]{0,1:T(8,128)} async-done(((f32[8192,384]{0,1:T(8,128)}), f32[2048,384]{0,1:T(8,128)}) %reduce-scatter.5.cloned.1.call-update) | async-done | bytes 3145744 | tf_op jit(solution)/shard_map/reduce_scatter | solution.py:15
  438.3 3.1 slice_bitcast_fusion
  441.4 1.3 copy.9
  442.7 1.3 copy.10
Async XLA Ops:
  7.2 40.6 %all-gather.14.cloned.1.call-start = ((), (), s32[]{:S(2)}) async-start(), calls=%async_computation.6 | async-start | bytes 2621440 | tf_op jit(solution)/shard_map/all_gather | solution.py:31
  7.9 88.4 %all-gather.10.cloned.1.call-start = ((), (), s32[]{:S(2)}) async-start(), calls=%async_computation.4 | async-start | bytes 4718592 | tf_op jit(solution)/shard_map/all_gather | solution.py:28
  8.6 123.5 %all-gather.12.cloned.1.call-start = ((), (), s32[]{:S(2)}) async-start(), calls=%async_computation.5 | async-start | bytes 2621440 | tf_op jit(solution)/shard_map/all_gather | solution.py:32
  9.4 159.6 %all-gather.8.cloned.1.call-start = ((), (), s32[]{:S(2)}) async-start(), calls=%async_computation.3 | async-start | bytes 2621440 | tf_op jit(solution)/shard_map/all_gather | solution.py:9
  10.0 207.4 %all-gather.6.cloned.1.call-start = ((), (), s32[]{:S(2)}) async-start(), calls=%async_computation.2 | async-start | bytes 4718592 | tf_op jit(solution)/shard_map/all_gather | solution.py:29
  10.5 305.5 %reduce-scatter.3.cloned.1.call-start = ((), (), s32[]{:S(2)}) async-start(), calls=%async_computation.7 | async-start | bytes 9437184 | tf_op jit(solution)/shard_map/reduce_scatter | solution.py:53
  136.2 85.3 %copy-start.1 = (bf16[8192,128]{1,0:T(8,128)(2,1)S(1)}, bf16[8192,128]{1,0:T(8,128)(2,1)}, u32[]{:S(2)}) copy-start(bf16[8192,128]{1,0:T(8,128)(2,1)} %all-gather.14.cloned.1.call-done) | copy-start | bytes 6291460
  221.5 1.6 copy-start.2
  227.6 210.7 %reduce-scatter.5.cloned.1.call-start = ((), (), s32[]{:S(2)}) async-start(), calls=%async_computation.8 | async-start | bytes 15728640 | tf_op jit(solution)/shard_map/reduce_scatter | solution.py:15
  227.6 3.5 copy-start
  231.1 2.9 copy-start.3
Sparse Core Ops, SparseCore 0:
  9.8 37.8 all-gather.13
  49.4 46.8 all-gather.9
  98.1 33.9 all-gather.11
  133.8 35.1 all-gather.7
  170.5 46.8 all-gather.5
  227.7 88.3 reduce-scatter.2
  319.2 119.0 reduce-scatter.4
where the time goes:
time: 451 us
  waiting for transfers between devices  398 us (88%)
  matrix products  22.8 us (5%)
  between operations  14.2 us (3%)
  local copies, waits for them, and re-layouts  8.46 us (2%)
  other arithmetic  7.1 us (2%)
    reduce_scatter x1, waiting for transfers between devices, own_rows(): lax.psum_scatter(portion(jnp.int32(0), count), axis, scatter_dimension=0,...  120 us
    reduce_scatter x1, waiting for transfers between devices, body(): lax.psum_scatter(partial_term, 'tp', scatter_dimension=1, tiled=True)  76.2 us
    all_gather x1, waiting for transfers between devices, body(): whole = lax.all_gather(tokens, 'tp', axis=1, tiled=True)  48.5 us
    all_gather x1, waiting for transfers between devices, body(): grads = lax.all_gather(out_grad, 'tp', axis=1, tiled=True)  48.4 us
    all_gather x1, waiting for transfers between devices, body(): lax.all_gather(gate_weight, 'fsdp', axis=0, tiled=True)  37.2 us
    all_gather x1, waiting for transfers between devices, over_all(): lax.all_gather(a, axis, axis=dim, tiled=True)  32.8 us
    all_gather x1, waiting for transfers between devices, body(): lax.all_gather(up_weight, 'fsdp', axis=0, tiled=True)  31.8 us
  transfers between devices with their start and end apart: 7, of which 7 were waited for; matrix products, arithmetic and copies ran while one was open for 4% of the time, Pallas kernels for 0%

commit v1 on v0

--- a/solution.py
+++ b/solution.py
@@ -3,6 +3,7 @@
 import jax.numpy as jnp
 from jax import lax
 from jax.sharding import PartitionSpec as P
+from jax.lax import axis_index, ppermute, psum
 
 
 def over_all(shard, axis, dim, absorb, state):
@@ -26,7 +27,15 @@
 def body(tokens, out_grad, gate_weight, up_weight, down_weight):
     factor = 1.0 / math.sqrt(tokens.shape[0] * lax.axis_size("fsdp"))
     whole = lax.all_gather(tokens, "tp", axis=1, tiled=True)
-    grads = lax.all_gather(out_grad, "tp", axis=1, tiled=True)
+    dev_count = psum(1, "tp")
+    reply = sorted(((u, (u + 1) % dev_count) for u in range(dev_count)))
+    e_now = out_grad
+    entries = [e_now]
+    for rr in range(1, dev_count):
+        e_now = ppermute(e_now, "tp", reply)
+        entries.insert(0, e_now)
+    out_arr = jnp.concatenate(entries, axis=1)
+    grads = jnp.roll(out_arr, shift=(axis_index("tp") + 1) * out_grad.shape[1], axis=1)
     gate_full, up_full = (
         lax.all_gather(gate_weight, "fsdp", axis=0, tiled=True),
         lax.all_gather(up_weight, "fsdp", axis=0, tiled=True),

time: 451 us -> 417 us (0.925)
  waiting for transfers between devices: 398 us -> 347 us
  local copies, waits for them, and re-layouts: 8.46 us -> 23.8 us
    ppermute x0 -> x7, waiting for transfers between devices: none -> 97.1 us  [body(): e_now = ppermute(e_now, 'tp', reply)]
    all_gather x1, waiting for transfers between devices: 48.5 us -> 0.01 us  [body(): whole = lax.all_gather(tokens, 'tp', axis=1, tiled=True)]
    all_gather x1 -> x0, waiting for transfers between devices: 48.4 us -> none  [body(): grads = lax.all_gather(out_grad, 'tp', axis=1, tiled=True)]
    all_gather x1, waiting for transfers between devices: 31.8 us -> 0.01 us  [body(): lax.all_gather(up_weight, 'fsdp', axis=0, tiled=True)]
    all_gather x1, waiting for transfers between devices: 37.2 us -> 15.7 us  [body(): lax.all_gather(gate_weight, 'fsdp', axis=0, tiled=True)]
    unnamed x10 -> x23, local copies, waits for them, and re-layouts: 5.38 us -> 19.9 us
  transfers between devices with their start and end apart: 7 -> 13, of which waited for: 7 -> 11; matrix products, arithmetic and copies ran while one was open for 4% -> 9% of each run, Pallas kernels for 0% -> 0%
where the time goes in v1:
time: 417 us
  waiting for transfers between devices  347 us (83%)
  matrix products  24.4 us (6%)
  local copies, waits for them, and re-layouts  23.8 us (6%)
  between operations  14.2 us (3%)
  other arithmetic  7.07 us (2%)
    reduce_scatter x1, waiting for transfers between devices, own_rows(): lax.psum_scatter(portion(jnp.int32(0), count), axis, scatter_dimension=0,...  120 us
    ppermute x7, waiting for transfers between devices, body(): e_now = ppermute(e_now, 'tp', reply)  97.1 us
    reduce_scatter x1, waiting for transfers between devices, body(): lax.psum_scatter(partial_term, 'tp', scatter_dimension=1, tiled=True)  79.6 us
    all_gather x1, waiting for transfers between devices, over_all(): lax.all_gather(a, axis, axis=dim, tiled=True)  32.8 us
    unnamed x23, local copies, waits for them, and re-layouts  19.9 us
    all_gather x1, waiting for transfers between devices, body(): lax.all_gather(gate_weight, 'fsdp', axis=0, tiled=True)  15.7 us
  transfers between devices with their start and end apart: 13, of which 11 were waited for; matrix products, arithmetic and copies ran while one was open for 9% of the time, Pallas kernels for 0%

profile of v1, /device:TPU:0, one launch (start us, length us, event | category | flops | bytes accessed | tf_op | source)
XLA Modules:
  0.0 417.0 jit_solution(7089358789763589093)
XLA Ops:
  7.2 0.0 copy-start.2
  7.2 0.0 all-gather.9.cloned.1.call-start
  7.2 0.7 all-gather.9.cloned.1.call-update
  7.9 0.0 all-gather.7.cloned.1.call-start
  8.0 0.7 all-gather.7.cloned.1.call-update
  8.7 0.0 all-gather.11.cloned.1.call-start
  8.7 0.5 collective-permute-start
  9.2 0.1 all-gather.11.cloned.1.call-update
  9.4 0.0 all-gather.5.cloned.1.call-start
  9.4 10.9 %collective-permute-done = bf16[256,1024]{1,0:T(8,128)(2,1)S(1)} collective-permute-done((bf16[256,1024]{1,0:T(8,128)(2,1)}, bf16[256,1024]{1,0:T(8,128)(2,1)S(1)}, u32[]{:S(2)}, u32[]{:S(2)}) %collective-permute-start) | collective-permute-done | bytes 524320 | tf_op jit(solution)/shard_map/ppermute | solution.py:35
  20.4 0.0 collective-permute-start.1
  20.4 10.4 %collective-permute-done.1 = bf16[256,1024]{1,0:T(8,128)(2,1)S(1)} collective-permute-done((bf16[256,1024]{1,0:T(8,128)(2,1)S(1)}, bf16[256,1024]{1,0:T(8,128)(2,1)S(1)}, u32[]{:S(2)}, u32[]{:S(2)}) %collective-permute-start.1) | collective-permute-done | bytes 524320 | tf_op jit(solution)/shard_map/ppermute | solution.py:35
  30.8 0.0 collective-permute-start.2
  30.8 10.4 %collective-permute-done.2 = bf16[256,1024]{1,0:T(8,128)(2,1)S(1)} collective-permute-done((bf16[256,1024]{1,0:T(8,128)(2,1)S(1)}, bf16[256,1024]{1,0:T(8,128)(2,1)S(1)}, u32[]{:S(2)}, u32[]{:S(2)}) %collective-permute-start.2) | collective-permute-done | bytes 524320 | tf_op jit(solution)/shard_map/ppermute | solution.py:35
  41.2 0.0 collective-permute-start.3
  41.2 10.4 %collective-permute-done.3 = bf16[256,1024]{1,0:T(8,128)(2,1)S(1)} collective-permute-done((bf16[256,1024]{1,0:T(8,128)(2,1)S(1)}, bf16[256,1024]{1,0:T(8,128)(2,1)S(1)}, u32[]{:S(2)}, u32[]{:S(2)}) %collective-permute-start.3) | collective-permute-done | bytes 524320 | tf_op jit(solution)/shard_map/ppermute | solution.py:35
  51.6 0.0 collective-permute-start.4
  51.6 11.1 %collective-permute-done.4 = bf16[256,1024]{1,0:T(8,128)(2,1)S(1)} collective-permute-done((bf16[256,1024]{1,0:T(8,128)(2,1)S(1)}, bf16[256,1024]{1,0:T(8,128)(2,1)S(1)}, u32[]{:S(2)}, u32[]{:S(2)}) %collective-permute-start.4) | collective-permute-done | bytes 524320 | tf_op jit(solution)/shard_map/ppermute | solution.py:35
  62.7 0.0 collective-permute-start.5
  62.7 21.9 %collective-permute-done.5 = bf16[256,1024]{1,0:T(8,128)(2,1)} collective-permute-done((bf16[256,1024]{1,0:T(8,128)(2,1)S(1)}, bf16[256,1024]{1,0:T(8,128)(2,1)}, u32[]{:S(2)}, u32[]{:S(2)}) %collective-permute-start.5) | collective-permute-done | bytes 524320 | tf_op jit(solution)/shard_map/ppermute | solution.py:35
  84.5 0.0 collective-permute-start.6
  84.5 0.0 all-gather.5.cloned.1.call-update
  84.6 0.0 reduce-scatter.3.cloned.1.call-start
  84.6 22.0 %collective-permute-done.6 = bf16[256,1024]{1,0:T(8,128)(2,1)} collective-permute-done((bf16[256,1024]{1,0:T(8,128)(2,1)}, bf16[256,1024]{1,0:T(8,128)(2,1)}, u32[]{:S(2)}, u32[]{:S(2)}) %collective-permute-start.6) | collective-permute-done | bytes 524320 | tf_op jit(solution)/shard_map/ppermute | solution.py:35
  106.6 1.9 constant_dynamic-update-slice_fusion.15
  108.5 1.9 constant_dynamic-update-slice_fusion.14
  110.4 0.9 constant_dynamic-update-slice_fusion.13
  111.2 0.8 constant_dynamic-update-slice_fusion.12
  112.1 0.8 constant_dynamic-update-slice_fusion.11
  112.9 0.9 constant_dynamic-update-slice_fusion.10
  113.8 0.8 constant_dynamic-update-slice_fusion.9
  114.6 0.0 copy-done.2
  114.6 0.9 constant_dynamic-update-slice_fusion.8
  115.5 1.9 constant_dynamic-update-slice_fusion.7
  117.4 1.9 constant_dynamic-update-slice_fusion.6
  119.4 0.9 constant_dynamic-update-slice_fusion.5
  120.2 0.8 constant_dynamic-update-slice_fusion.4
  121.1 0.8 constant_dynamic-update-slice_fusion.3
  121.9 0.8 constant_dynamic-update-slice_fusion.2
  122.8 0.9 constant_dynamic-update-slice_fusion.1
  123.6 0.9 constant_dynamic-update-slice_fusion
  124.5 4.1 fusion.10
  128.6 15.7 %all-gather.11.cloned.1.call-done = bf16[8192,128]{1,0:T(8,128)(2,1)} async-done(((bf16[2048,128]{1,0:T(8,128)(2,1)}), bf16[8192,128]{1,0:T(8,128)(2,1)}) %all-gather.11.cloned.1.call-update) | async-done | bytes 2097168 | tf_op jit(solution)/shard_map/all_gather | solution.py:40
  144.3 4.1 fusion.11
  148.4 0.0 copy-start.1
  148.4 32.8 %all-gather.5.cloned.1.call-done = bf16[128,8192]{1,0:T(8,128)(2,1)} async-done(((bf16[128,2048]{1,0:T(8,128)(2,1)}), bf16[128,8192]{1,0:T(8,128)(2,1)}) %all-gather.5.cloned.1.call-update) | async-done | bytes 2097168 | tf_op jit(solution)/shard_map/all_gather | solution.py:10
  181.2 4.1 multiply_convert_fusion.1
  185.3 2.8 fusion.12
  188.2 0.0 copy-done.1
  188.2 4.5 %convolution_add_fusion = f32[256,8192]{1,0:T(8,128)} fusion(f32[256,8192]{1,0:T(8,128)S(1)} %fusion.12, bf16[256,128]{1,0:T(8,128)(2,1)S(1)} %get-tuple-element.11, bf16[8192,128]{1,0:T(8,128)(2,1)S(1)} %copy-done.1), kind=kOutput, calls=%fused_computation.1 | convolution fusion | flops 538968064 | bytes 18939904 | tf_op jit(solution)/shard_map/dot_general | solution.py:61
  192.7 0.0 reduce-scatter.3.cloned.1.call-update
  192.7 0.0 reduce-scatter.5.cloned.1.call-start
  192.8 3.2 convolution_multiply_fusion
  196.0 0.3 copy-done
  196.2 0.8 fusion
  197.0 0.8 fusion.1
  197.8 5.0 %pad_maximum_fusion = f32[8192,384]{0,1:T(8,128)} fusion(f32[8192,128]{0,1:T(8,128)S(1)} %convolution_multiply_fusion, f32[8192,128]{0,1:T(8,128)S(1)} %fusion, f32[8192,128]{0,1:T(8,128)S(1)} %fusion.1), kind=kLoop, calls=%fused_computation | loop fusion | flops 6291456 | bytes 25165824 | tf_op jit(solution)/shard_map/concatenate | solution.py:68
  202.8 0.0 reduce-scatter.5.cloned.1.call-update
  202.8 79.6 %reduce-scatter.3.cloned.1.call-done = f32[256,1024]{1,0:T(8,128)} async-done(((f32[256,8192]{1,0:T(8,128)}), f32[256,1024]{1,0:T(8,128)}) %reduce-scatter.3.cloned.1.call-update) | async-done | bytes 1048592 | tf_op jit(solution)/shard_map/reduce_scatter | solution.py:62
  282.4 2.1 convert_element_type.14
  284.5 120.0 %reduce-scatter.5.cloned.1.call-done = f32[2048,384]{0,1:T(8,128)} async-done(((f32[8192,384]{0,1:T(8,128)}), f32[2048,384]{0,1:T(8,128)}) %reduce-scatter.5.cloned.1.call-update) | async-done | bytes 3145744 | tf_op jit(solution)/shard_map/reduce_scatter | solution.py:16
  404.5 3.1 slice_bitcast_fusion
  407.5 1.3 copy.10
  408.8 1.3 copy.9
  (3 shorter events, 0.0 us)
Async XLA Ops:
  7.2 107.5 %copy-start.2 = (bf16[256,1024]{1,0:T(8,128)(2,1)S(1)}, bf16[256,1024]{1,0:T(8,128)(2,1)}, u32[]{:S(2)}) copy-start(bf16[256,1024]{1,0:T(8,128)(2,1)} %param.6) | copy-start | bytes 1572868
  7.2 117.3 %all-gather.9.cloned.1.call-start = ((), (), s32[]{:S(2)}) async-start(), calls=%async_computation.4 | async-start | bytes 2621440 | tf_op jit(solution)/shard_map/all_gather | solution.py:41
  7.9 116.6 %all-gather.7.cloned.1.call-start = ((), (), s32[]{:S(2)}) async-start(), calls=%async_computation.3 | async-start | bytes 4718592 | tf_op jit(solution)/shard_map/all_gather | solution.py:29
  8.7 135.6 %all-gather.11.cloned.1.call-start = ((), (), s32[]{:S(2)}) async-start(), calls=%async_computation.5 | async-start | bytes 2621440 | tf_op jit(solution)/shard_map/all_gather | solution.py:40
  8.7 11.6 %collective-permute-start = (bf16[256,1024]{1,0:T(8,128)(2,1)}, bf16[256,1024]{1,0:T(8,128)(2,1)S(1)}, u32[]{:S(2)}, u32[]{:S(2)}) collective-permute-start(bf16[256,1024]{1,0:T(8,128)(2,1)} %param.6), channel_id=1, source_target_pairs={{0,1},{1,2},{2,3},{3,4},{4,5},{5,6},{6,7},{7,0},{8,9},{9,10},{10,1... | collective-permute-start | bytes 1572872 | tf_op jit(solution)/shard_map/ppermute | solution.py:35
  9.4 171.8 %all-gather.5.cloned.1.call-start = ((), (), s32[]{:S(2)}) async-start(), calls=%async_computation.2 | async-start | bytes 2621440 | tf_op jit(solution)/shard_map/all_gather | solution.py:10
  20.4 10.4 %collective-permute-start.1 = (bf16[256,1024]{1,0:T(8,128)(2,1)S(1)}, bf16[256,1024]{1,0:T(8,128)(2,1)S(1)}, u32[]{:S(2)}, u32[]{:S(2)}) collective-permute-start(bf16[256,1024]{1,0:T(8,128)(2,1)S(1)} %collective-permute-done), channel_id=1, source_target_pairs={{0,1},{1,2},{2,3},{3,4},{4,5},{5,6},{6,7},{7,0},{8,9},{9,10},{10,1... | collective-permute-start | bytes 1572872 | tf_op jit(solution)/shard_map/ppermute | solution.py:35
  30.8 10.4 %collective-permute-start.2 = (bf16[256,1024]{1,0:T(8,128)(2,1)S(1)}, bf16[256,1024]{1,0:T(8,128)(2,1)S(1)}, u32[]{:S(2)}, u32[]{:S(2)}) collective-permute-start(bf16[256,1024]{1,0:T(8,128)(2,1)S(1)} %collective-permute-done.1), channel_id=1, source_target_pairs={{0,1},{1,2},{2,3},{3,4},{4,5},{5,6},{6,7},{7,0},{8,9},{9,10},{10,1... | collective-permute-start | bytes 1572872 | tf_op jit(solution)/shard_map/ppermute | solution.py:35
  41.2 10.4 %collective-permute-start.3 = (bf16[256,1024]{1,0:T(8,128)(2,1)S(1)}, bf16[256,1024]{1,0:T(8,128)(2,1)S(1)}, u32[]{:S(2)}, u32[]{:S(2)}) collective-permute-start(bf16[256,1024]{1,0:T(8,128)(2,1)S(1)} %collective-permute-done.2), channel_id=1, source_target_pairs={{0,1},{1,2},{2,3},{3,4},{4,5},{5,6},{6,7},{7,0},{8,9},{9,10},{10,1... | collective-permute-start | bytes 1572872 | tf_op jit(solution)/shard_map/ppermute | solution.py:35
  51.6 11.1 %collective-permute-start.4 = (bf16[256,1024]{1,0:T(8,128)(2,1)S(1)}, bf16[256,1024]{1,0:T(8,128)(2,1)S(1)}, u32[]{:S(2)}, u32[]{:S(2)}) collective-permute-start(bf16[256,1024]{1,0:T(8,128)(2,1)S(1)} %collective-permute-done.3), channel_id=1, source_target_pairs={{0,1},{1,2},{2,3},{3,4},{4,5},{5,6},{6,7},{7,0},{8,9},{9,10},{10,1... | collective-permute-start | bytes 1572872 | tf_op jit(solution)/shard_map/ppermute | solution.py:35
  62.7 21.9 %collective-permute-start.5 = (bf16[256,1024]{1,0:T(8,128)(2,1)S(1)}, bf16[256,1024]{1,0:T(8,128)(2,1)}, u32[]{:S(2)}, u32[]{:S(2)}) collective-permute-start(bf16[256,1024]{1,0:T(8,128)(2,1)S(1)} %collective-permute-done.4), channel_id=1, source_target_pairs={{0,1},{1,2},{2,3},{3,4},{4,5},{5,6},{6,7},{7,0},{8,9},{9,10},{10,1... | collective-permute-start | bytes 1572872 | tf_op jit(solution)/shard_map/ppermute | solution.py:35
  84.5 22.1 %collective-permute-start.6 = (bf16[256,1024]{1,0:T(8,128)(2,1)}, bf16[256,1024]{1,0:T(8,128)(2,1)}, u32[]{:S(2)}, u32[]{:S(2)}) collective-permute-start(bf16[256,1024]{1,0:T(8,128)(2,1)} %collective-permute-done.5), channel_id=1, source_target_pairs={{0,1},{1,2},{2,3},{3,4},{4,5},{5,6},{6,7},{7,0},{8,9},{9,10},{10,1... | collective-permute-start | bytes 1572872 | tf_op jit(solution)/shard_map/ppermute | solution.py:35
  84.6 197.8 %reduce-scatter.3.cloned.1.call-start = ((), (), s32[]{:S(2)}) async-start(), calls=%async_computation.6 | async-start | bytes 9437184 | tf_op jit(solution)/shard_map/reduce_scatter | solution.py:62
  148.4 39.8 %copy-start.1 = (bf16[8192,128]{1,0:T(8,128)(2,1)S(1)}, bf16[8192,128]{1,0:T(8,128)(2,1)}, u32[]{:S(2)}) copy-start(bf16[8192,128]{1,0:T(8,128)(2,1)} %all-gather.9.cloned.1.call-done) | copy-start | bytes 6291460
  192.7 211.8 %reduce-scatter.5.cloned.1.call-start = ((), (), s32[]{:S(2)}) async-start(), calls=%async_computation.7 | async-start | bytes 15728640 | tf_op jit(solution)/shard_map/reduce_scatter | solution.py:16
  192.8 3.5 copy-start
Sparse Core Ops, SparseCore 0:
  9.8 37.8 all-gather.8
  49.4 59.2 all-gather.6
  110.5 33.7 all-gather.10
  146.0 35.1 all-gather.4
  192.8 89.5 reduce-scatter.2
  285.3 119.0 reduce-scatter.4
